TPU v7x, 256 devices: a whole 4x4x8 slice. The times are simulated.
256 devices in a mesh: grp: 4 (over y), col: 64 (over x, z, core).
Axes of the slice: x: 4, y: 4, z: 8, core: 2. Of those that a mesh axis runs over, the one named last changes fastest.
Arguments:
- panels: bfloat16 [256, 4, 512, 512], P('col', None, 'grp'), may hold values from -1.296875 to 1.296875
- parent: float32 [256, 512, 512], P('col', 'grp'), may hold values from -6 to 6
- src_block: int32 [64, 40], P('col'), may hold values from 0 to 39, each once within a row
- dest_owner: int32 [2560, 1], P('col'), may hold values from 0 to 63; in each aligned block of 40 rows (0 to 39, 40 to 79, ...) no two rows name the same one
- target: int32 [2560], P('col'), may hold values from 0 to 3
- counts: int32 [64], P('col'), may hold values from 20 to 40, as said below
Outputs:
- assembled: float32 [256, 512, 512], P('col', 'grp')
Inputs may be any that keep to these rules, and one draw needn't show every extreme that they name: `src_block`: each row of a column rank is a permutation of the 40 block pairs. `dest_owner`: among the 40 slots of one column rank at most 1 name the same owner. The live slots of a rank are its first counts[c]; some rank has all 40 live.
All inputs are finite; a program needn't handle non-finite values.
Results may differ from a plain program's by a relative error of at most 0.0026.
Values may be sent and summed in bfloat16 or wider, within the bound.
A program may use at most 128 MiB of HBM per device.

v0:
```python
import jax
import jax.numpy as jnp
import numpy as np
from jax import lax
from jax.sharding import PartitionSpec as P


def place_slots(src_block, dest_owner, target, counts, peer_count, capacity):
    slot_count = src_block.shape[1]
    slot_index = jnp.arange(slot_count, dtype=jnp.int32)
    owner_rank = dest_owner[:, 0]
    matches = (owner_rank[:, None] == jnp.arange(peer_count, dtype=jnp.int32)[None, :]).astype(
        jnp.int32
    )
    earlier = jnp.cumsum(matches, axis=0) - matches
    rank_in = jnp.sum(earlier * matches, axis=1)
    position = owner_rank * capacity + rank_in
    is_live = slot_index < counts[0]
    routed = jnp.zeros((peer_count * capacity,), jnp.int32).at[position].set(target)
    return (src_block[0], position, is_live, routed.reshape(peer_count, capacity))


def pack_updates(flat_updates, chosen, position, is_live, peer_count, capacity):
    picked = flat_updates[chosen]
    picked = jnp.where(is_live[:, None, None], picked, jnp.zeros_like(picked))
    buffer = (
        jnp.zeros((peer_count * capacity,) + picked.shape[1:], picked.dtype)
        .at[position]
        .set(picked)
    )
    return buffer.reshape((peer_count, capacity) + picked.shape[1:])


def assemble(received, labels, targets):
    arrived = received.reshape((-1,) + received.shape[2:])
    flat_labels = labels.reshape(-1)
    select = (flat_labels[None, :] == jnp.arange(targets, dtype=jnp.int32)[:, None]).astype(
        jnp.bfloat16
    )
    return jnp.einsum("tn,nrc->trc", select, arrived, preferred_element_type=jnp.float32)


def pair_products(own_rows, piece_rows):
    blocks = own_rows.shape[1]
    upper_table = np.array([a for a in range(blocks) for b in range(a + 1)], np.int32)
    lower_table = np.array([b for a in range(blocks) for b in range(a + 1)], np.int32)
    left_rows = own_rows[:, upper_table]
    right_rows = piece_rows[:, lower_table]
    return jnp.einsum(
        "fprw,fpcw->fprc", left_rows, right_rows, preferred_element_type=jnp.float32
    ).astype(jnp.bfloat16)


def per_device(panels, parent, src_block, dest_owner, target, counts):
    fronts, blocks, quarter, _ = panels.shape
    pair_count = blocks * (blocks + 1) // 2
    peer_count = lax.axis_size("col")
    slot_count = src_block.shape[1]
    capacity = (slot_count + peer_count - 1) // peer_count + slot_count // (2 * peer_count)
    targets = parent.shape[0]
    chosen, position, is_live, routed = place_slots(
        src_block, dest_owner, target, counts, peer_count, capacity
    )
    products = pair_products(panels, lax.all_gather(panels, "grp", axis=2, tiled=True))
    flat_updates = products.reshape(fronts * pair_count, quarter, products.shape[3])
    buffer = pack_updates(flat_updates, chosen, position, is_live, peer_count, capacity)
    received, labels = (
        lax.all_to_all(buffer, "col", split_axis=0, concat_axis=0, tiled=True),
        lax.all_to_all(routed, "col", split_axis=0, concat_axis=0, tiled=True),
    )
    return parent - assemble(received, labels, targets)


def solution(mesh):
    placed = (
        P("col", None, "grp", None),
        P("col", "grp", None),
        P("col", None),
        P("col", None),
        P("col"),
        P("col"),
    )
    return jax.shard_map(
        per_device, mesh=mesh, in_specs=placed, out_specs=P("col", "grp", None), check_vma=False
    )
```

profile of v0, /device:TPU:1, one launch (start us, length us, event | category | flops | bytes accessed | tf_op | source)
XLA Modules:
  0.0 390.6 jit_solution(11302547754613624316)
XLA Ops:
  6.5 0.0 copy-start.1
  6.5 0.0 copy-start.2
  6.5 0.0 all-gather.2.cloned.1.call-start
  6.5 0.7 all-gather.2.cloned.1.call-update
  7.3 0.7 fusion.13
  8.0 0.1 reduce_window_sum.11
  8.1 0.8 select_reduce_fusion
  8.9 0.7 fusion.17
  9.6 0.8 scatter_custom_fusion
  10.4 0.7 copy.36
  11.1 13.0 %all-to-all-start = ((s32[64,1,1]{2,1,0:T(1,128)}), s32[64,1,1]{2,1,0:T(1,128)S(1)}, u32[]{:S(2)}, u32[]{:S(2)}) async-start(s32[64,1,1]{2,1,0:T(1,128)} %copy.36), calls=%async_computation | async-start | bytes 65536 | tf_op jit(solution)/shard_map/all_to_all | solution.py:69
  24.1 0.7 pad_clamp_fusion.2
  24.8 5.7 %gather_fusion = bf16[10,4,128,512]{3,2,1,0:T(8,128)(2,1)} fusion(bf16[4,4,128,512]{3,2,1,0:T(8,128)(2,1)} %param.10, s32[1024]{0:T(1024)S(1)} %pad_clamp_fusion.2), kind=kCustom, calls=%fused_computation | custom fusion | bytes 10485800 | tf_op jit(solution)/shard_map/gather | solution.py:47
  31.1 0.0 copy-done.1
  31.1 0.0 copy-done.2
  31.2 67.3 %all-gather.2.cloned.1.call-done = bf16[4,4,512,512]{3,2,1,0:T(8,128)(2,1)} async-done(((bf16[4,4,128,512]{3,2,1,0:T(8,128)(2,1)}), bf16[4,4,512,512]{3,2,1,0:T(8,128)(2,1)}) %all-gather.2.cloned.1.call-update) | async-done | bytes 8388624 | tf_op jit(solution)/shard_map/all_gather | solution.py:64
  98.4 6.0 %fusion.22 = (bf16[4,4,256,512]{3,2,1,0:T(8,128)(2,1)}, bf16[4,4,256,512]{3,2,1,0:T(8,128)(2,1)}) fusion(bf16[4,4,512,512]{3,2,1,0:T(8,128)(2,1)} %all-gather.2.cloned.1.call-done), kind=kLoop, calls=%fused_computation.37 | loop fusion | bytes 16777216 | tf_op jit(solution)/shard_map/gather | solution.py:48
  104.5 7.6 %gather_fusion.2 = bf16[10,4,256,512]{3,2,1,0:T(8,128)(2,1)} fusion(bf16[4,4,256,512]{3,2,1,0:T(8,128)(2,1)} %get-tuple-element.5, s32[1024]{0:T(1024)S(1)} %pad_clamp_fusion.1), kind=kCustom, calls=%fused_computation.2 | custom fusion | bytes 20971560 | tf_op jit(solution)/shard_map/gather | solution.py:48
  112.1 0.0 slice-start
  112.1 7.7 %gather_fusion.3 = bf16[10,4,256,512]{3,2,1,0:T(8,128)(2,1)} fusion(bf16[4,4,256,512]{3,2,1,0:T(8,128)(2,1)} %get-tuple-element.6, s32[1024]{0:T(1024)S(1)} %pad_clamp_fusion.1), kind=kCustom, calls=%fused_computation.3 | custom fusion | bytes 20971560 | tf_op jit(solution)/shard_map/gather | solution.py:48
  119.7 0.0 slice-start.1
  119.7 12.3 %copy_bitcast_fusion = (bf16[4,10,256,512]{3,2,1,0:T(8,128)(2,1)S(1)}, bf16[4,10,256,512]{3,2,1,0:T(8,128)(2,1)}) fusion(bf16[10,4,256,512]{3,2,1,0:T(8,128)(2,1)} %gather_fusion.3, bf16[10,4,256,512]{3,2,1,0:T(8,128)(2,1)} %gather_fusion.2), kind=kLoop, calls=%fused_computation.10 | loop fusion | bytes 41943040 | tf_op jit(solution)/shard_map/gather | solution.py:48
  132.1 0.0 slice-done
  132.1 0.0 slice-done.1
  132.1 10.5 %fusion.8 = bf16[4,10,128,512]{3,2,1,0:T(8,128)(2,1)} fusion(bf16[4,10,256,512]{3,2,1,0:T(8,128)(2,1)S(1)} %get-tuple-element.7, bf16[4,10,256,512]{3,2,1,0:T(8,128)(2,1)} %get-tuple-element.8, bf16[10,4,128,512]{3,2,1,0:T(8,128)(2,1)S(1)} %bitcast.34), kind=kOutput, calls=%fused_computation.17 | convolution fusion | flops 2728919040 | bytes 31457280 | tf_op jit(solution)/shard_map/fprw,fpcw->fprc/dot_general | solution.py:49
  142.6 7.2 %gather_fusion.1 = bf16[40,128,512]{2,1,0:T(8,128)(2,1)} fusion(bf16[40,128,512]{2,1,0:T(8,128)(2,1)} %bitcast.35, s32[1024]{0:T(1024)S(1)} %pad_clamp_fusion), kind=kCustom, calls=%fused_computation.1 | custom fusion | bytes 10485920 | tf_op jit(solution)/shard_map/gather | solution.py:24
  149.8 5.3 %broadcast_select_fusion = bf16[40,128,512]{2,1,0:T(8,128)(2,1)} fusion(bf16[40,128,512]{2,1,0:T(8,128)(2,1)} %gather_fusion.1, pred[40]{0:T(512)(128)(4,1)S(1)} %iota_compare_fusion.2), kind=kLoop, calls=%fused_computation.16 | loop fusion | flops 2621440 | bytes 10485800 | tf_op jit(solution)/shard_map/jit(_where)/select_n | solution.py:25
  155.1 4.2 %broadcast_in_dim.30 = bf16[64,128,512]{2,1,0:T(8,128)(2,1)} broadcast(bf16[]{:T(256)} %constant.10.clone.1), dimensions={} | broadcast | bytes 8388610 | tf_op jit(solution)/shard_map/broadcast_in_dim | solution.py:27
  159.3 14.1 %scatter_fusion = bf16[64,128,512]{2,1,0:T(8,128)(2,1)} fusion(bf16[64,128,512]{2,1,0:T(8,128)(2,1)} %broadcast_in_dim.30, s32[40]{0:T(128)S(1)} %fusion.17, bf16[40,128,512]{2,1,0:T(8,128)(2,1)} %broadcast_select_fusion), kind=kCustom, calls=%fused_computation.5 | custom fusion | bytes 15728800 | tf_op jit(solution)/shard_map/scatter | solution.py:29
  173.4 0.0 all-to-all-done
  173.4 11.0 %all-to-all-start.1 = ((bf16[64,1,128,512]{3,2,1,0:T(8,128)(2,1)}), bf16[64,1,128,512]{3,2,1,0:T(8,128)(2,1)}, u32[]{:S(2)}, u32[]{:S(2)}) async-start(bf16[64,1,128,512]{3,2,1,0:T(8,128)(2,1)} %bitcast.32), calls=%async_computation.1 | async-start | bytes 16777216 | tf_op jit(solution)/shard_map/all_to_all | solution.py:68
  184.3 0.0 copy-start
  184.4 1.2 reduce
  185.6 184.5 %all-to-all-done.1 = bf16[64,1,128,512]{3,2,1,0:T(8,128)(2,1)} async-done(((bf16[64,1,128,512]{3,2,1,0:T(8,128)(2,1)}), bf16[64,1,128,512]{3,2,1,0:T(8,128)(2,1)}, u32[]{:S(2)}, u32[]{:S(2)}) %all-to-all-start.1) | async-done | bytes 8388640 | tf_op jit(solution)/shard_map/all_to_all | solution.py:68
  370.1 12.3 %fusion.4 = f32[4,128,512]{2,0,1:T(4,128)S(1)} fusion(bf16[64,1,128,512]{3,2,1,0:T(8,128)(2,1)} %all-to-all-done.1, s32[64]{0:T(128)S(1)} %reduce), kind=kOutput, calls=%fused_computation.12 | convolution fusion | flops 33554688 | bytes 9437440 | tf_op jit(solution)/shard_map/tn,nrc->trc/dot_general | solution.py:40
  382.3 0.0 copy-done
  382.3 1.4 copy_subtract_fusion
  (5 shorter events, 0.0 us)
Async XLA Ops:
  6.5 24.6 %copy-start.1 = (s32[10]{0:T(128)S(1)}, s32[10]{0:T(128)}, u32[]{:S(2)}) copy-start(s32[10]{0:T(128)} %constant.35) | copy-start | bytes 124
  6.5 24.6 %copy-start.2 = (s32[1,40]{1,0:T(1,128)S(1)}, s32[1,40]{1,0:T(1,128)}, u32[]{:S(2)}) copy-start(s32[1,40]{1,0:T(1,128)} %param.12) | copy-start | bytes 484
  6.5 91.9 %all-gather.2.cloned.1.call-start = ((), (), s32[]{:S(2)}) async-start(), calls=%async_computation.2 | async-start | bytes 10485760 | tf_op jit(solution)/shard_map/all_gather | solution.py:64
  11.1 162.3 %all-to-all-start = ((s32[64,1,1]{2,1,0:T(1,128)}), s32[64,1,1]{2,1,0:T(1,128)S(1)}, u32[]{:S(2)}, u32[]{:S(2)}) async-start(s32[64,1,1]{2,1,0:T(1,128)} %copy.36), calls=%async_computation | async-start | bytes 65536 | tf_op jit(solution)/shard_map/all_to_all | solution.py:69
  112.1 20.0 %slice-start = ((s8[5242880]{0:T(1024)(128)(4,1)}), s8[1048576]{0:T(1024)(128)(4,1)S(1)}, s32[]{:S(2)}) async-start(s8[5242880]{0:T(1024)(128)(4,1)} %bitcast.33), calls=%async_computation.3 | async-start | bytes 2097152
  119.7 12.4 %slice-start.1 = ((s8[5242880]{0:T(1024)(128)(4,1)}), s8[4194304]{0:T(1024)(128)(4,1)S(1)}, s32[]{:S(2)}) async-start(s8[5242880]{0:T(1024)(128)(4,1)} %bitcast.33), calls=%async_computation.4 | async-start | bytes 8388608
  173.4 196.7 %all-to-all-start.1 = ((bf16[64,1,128,512]{3,2,1,0:T(8,128)(2,1)}), bf16[64,1,128,512]{3,2,1,0:T(8,128)(2,1)}, u32[]{:S(2)}, u32[]{:S(2)}) async-start(bf16[64,1,128,512]{3,2,1,0:T(8,128)(2,1)} %bitcast.32), calls=%async_computation.1 | async-start | bytes 16777216 | tf_op jit(solution)/shard_map/all_to_all | solution.py:68
  184.3 198.0 %copy-start = (f32[4,128,512]{2,1,0:T(8,128)S(1)}, f32[4,128,512]{2,1,0:T(8,128)}, u32[]{:S(2)}) copy-start(f32[4,128,512]{2,1,0:T(8,128)} %param.11) | copy-start | bytes 3145732
Sparse Core Ops, SparseCore 0:
  9.1 89.2 all-gather.1
where the time goes:
time: 391 us
  waiting for transfers between devices  252 us (64%)
  local copies, waits for them, and re-layouts  66.4 us (17%)
  starting transfers between devices  23.9 us (6%)
  matrix products  22.8 us (6%)
  between operations  14.1 us (4%)
  other arithmetic  10.9 us (3%)
    all_to_all x1, waiting for transfers between devices, per_device(): lax.all_to_all(buffer, 'col', split_axis=0, concat_axis=0, tiled=True)  184 us
    all_gather x1, waiting for transfers between devices, per_device(): lax.all_gather(panels, 'grp', axis=2, tiled=True)  67.3 us
    gather x4, local copies, waits for them, and re-layouts, pair_products(): right_rows = piece_rows[:, lower_table]  33.6 us
    scatter x1, local copies, waits for them, and re-layouts, pack_updates(): buffer = jnp.zeros((peer_count * capacity,) + picked.shape[1:], picked.dt...  14.1 us
    all_to_all x1, starting transfers between devices, per_device(): lax.all_to_all(routed, 'col', split_axis=0, concat_axis=0, tiled=True)  13 us
    dot_general x1, matrix products, assemble(): jnp.einsum('tn,nrc->trc', select, arrived, preferred_element_type=jnp.flo...  12.3 us
    all_to_all x1, starting transfers between devices, per_device(): lax.all_to_all(buffer, 'col', split_axis=0, concat_axis=0, tiled=True)  11 us
    dot_general x1, matrix products, pair_products(): jnp.einsum('fprw,fpcw->fprc', left_rows, right_rows, preferred_element_ty...  10.5 us
  transfers between devices with their start and end apart: 3, of which 2 were waited for; matrix products, arithmetic and copies ran while one was open for 22% of the time, Pallas kernels for 0%

commit v1 on v0

--- a/solution.py
+++ b/solution.py
@@ -3,6 +3,11 @@
 import numpy as np
 from jax import lax
 from jax.sharding import PartitionSpec as P
+
+
+def all_parts(x, axis, dim):
+    pieces = lax.all_gather(x, axis)
+    return jnp.concatenate(pieces, axis=dim)
 
 
 def place_slots(src_block, dest_owner, target, counts, peer_count, capacity):
@@ -61,7 +66,7 @@
     chosen, position, is_live, routed = place_slots(
         src_block, dest_owner, target, counts, peer_count, capacity
     )
-    products = pair_products(panels, lax.all_gather(panels, "grp", axis=2, tiled=True))
+    products = pair_products(panels, all_parts(panels, "grp", 2))
     flat_updates = products.reshape(fronts * pair_count, quarter, products.shape[3])
     buffer = pack_updates(flat_updates, chosen, position, is_live, peer_count, capacity)
     received, labels = (

time: 391 us -> 399 us (1.020)
  local copies, waits for them, and re-layouts: 66.4 us -> 73.8 us
    reshape x0 -> x1, local copies, waits for them, and re-layouts: none -> 7.6 us  [all_parts(): return jnp.concatenate(pieces, axis=dim)]
  transfers between devices with their start and end apart: 3 -> 3, of which waited for: 2 -> 2; matrix products, arithmetic and copies ran while one was open for 22% -> 24% of each run, Pallas kernels for 0% -> 0%
where the time goes in v1:
time: 399 us; the launch traced here: 398 us
  waiting for transfers between devices  252 us (63%)
  local copies, waits for them, and re-layouts  73.8 us (18%)
  starting transfers between devices  24 us (6%)
  matrix products  22.8 us (6%)
  between operations  14.1 us (4%)
  other arithmetic  10.9 us (3%)
    all_to_all x1, waiting for transfers between devices, per_device(): lax.all_to_all(buffer, 'col', split_axis=0, concat_axis=0, tiled=True)  184 us
    all_gather x1, waiting for transfers between devices, all_parts(): pieces = lax.all_gather(x, axis)  67.3 us
    gather x4, local copies, waits for them, and re-layouts, pair_products(): right_rows = piece_rows[:, lower_table]  33.4 us
    scatter x1, local copies, waits for them, and re-layouts, pack_updates(): buffer = jnp.zeros((peer_count * capacity,) + picked.shape[1:], picked.dt...  14.1 us
    all_to_all x1, starting transfers between devices, per_device(): lax.all_to_all(routed, 'col', split_axis=0, concat_axis=0, tiled=True)  13 us
    dot_general x1, matrix products, assemble(): jnp.einsum('tn,nrc->trc', select, arrived, preferred_element_type=jnp.flo...  12.3 us
    all_to_all x1, starting transfers between devices, per_device(): lax.all_to_all(buffer, 'col', split_axis=0, concat_axis=0, tiled=True)  11 us
    dot_general x1, matrix products, pair_products(): jnp.einsum('fprw,fpcw->fprc', left_rows, right_rows, preferred_element_ty...  10.5 us
  transfers between devices with their start and end apart: 3, of which 2 were waited for; matrix products, arithmetic and copies ran while one was open for 24% of the time, Pallas kernels for 0%

profile of v1, /device:TPU:1, one launch (start us, length us, event | category | flops | bytes accessed | tf_op | source)
XLA Modules:
  0.0 398.0 jit_solution(4954429753130246199)
XLA Ops:
  6.5 0.0 copy-start.1
  6.5 0.0 copy-start.2
  6.5 0.0 all-gather.3.cloned.1.call-start
  6.5 0.7 all-gather.3.cloned.1.call-update
  7.3 0.7 fusion.13
  8.0 0.1 reduce_window_sum.11
  8.1 0.8 select_reduce_fusion
  8.9 0.7 fusion.17
  9.6 0.8 scatter_custom_fusion
  10.4 0.7 copy.45
  11.1 13.0 %all-to-all-start = ((s32[64,1,1]{2,1,0:T(1,128)}), s32[64,1,1]{2,1,0:T(1,128)S(1)}, u32[]{:S(2)}, u32[]{:S(2)}) async-start(s32[64,1,1]{2,1,0:T(1,128)} %copy.45), calls=%async_computation | async-start | bytes 65536 | tf_op jit(solution)/shard_map/all_to_all | solution.py:74
  24.1 0.7 pad_clamp_fusion.2
  24.8 5.7 %gather_fusion = bf16[10,4,128,512]{3,2,1,0:T(8,128)(2,1)} fusion(bf16[4,4,128,512]{3,2,1,0:T(8,128)(2,1)} %param.10, s32[1024]{0:T(1024)S(1)} %pad_clamp_fusion.2), kind=kCustom, calls=%fused_computation | custom fusion | bytes 10485800 | tf_op jit(solution)/shard_map/gather | solution.py:52
  31.1 0.0 copy-done.1
  31.1 0.0 copy-done.2
  31.2 67.3 %all-gather.3.cloned.1.call-done = bf16[16,4,128,512]{3,2,1,0:T(8,128)(2,1)} async-done(((bf16[4,4,128,512]{3,2,1,0:T(8,128)(2,1)}), bf16[16,4,128,512]{3,2,1,0:T(8,128)(2,1)}) %all-gather.3.cloned.1.call-update) | async-done | bytes 8388624 | tf_op jit(solution)/shard_map/all_gather | solution.py:9
  98.4 7.6 %copy.46 = bf16[4,4,4,128,512]{4,3,2,1,0:T(8,128)(2,1)} copy(bf16[4,4,4,128,512]{4,3,1,0,2:T(8,128)(2,1)} %bitcast.38) | data formatting | bytes 16777216 | tf_op jit(solution)/shard_map/reshape | solution.py:10
  106.0 5.8 %fusion.22 = (bf16[4,4,256,512]{3,2,1,0:T(8,128)(2,1)}, bf16[4,4,256,512]{3,2,1,0:T(8,128)(2,1)}) fusion(bf16[4,4,512,512]{3,2,1,0:T(8,128)(2,1)} %bitcast.37), kind=kLoop, calls=%fused_computation.37 | loop fusion | bytes 16777216 | tf_op jit(solution)/shard_map/gather | solution.py:53
  111.8 7.6 %gather_fusion.2 = bf16[10,4,256,512]{3,2,1,0:T(8,128)(2,1)} fusion(bf16[4,4,256,512]{3,2,1,0:T(8,128)(2,1)} %get-tuple-element.5, s32[1024]{0:T(1024)S(1)} %pad_clamp_fusion.1), kind=kCustom, calls=%fused_computation.2 | custom fusion | bytes 20971560 | tf_op jit(solution)/shard_map/gather | solution.py:53
  119.5 0.0 slice-start
  119.5 7.7 %gather_fusion.3 = bf16[10,4,256,512]{3,2,1,0:T(8,128)(2,1)} fusion(bf16[4,4,256,512]{3,2,1,0:T(8,128)(2,1)} %get-tuple-element.6, s32[1024]{0:T(1024)S(1)} %pad_clamp_fusion.1), kind=kCustom, calls=%fused_computation.3 | custom fusion | bytes 20971560 | tf_op jit(solution)/shard_map/gather | solution.py:53
  127.1 0.0 slice-start.1
  127.1 12.3 %copy_bitcast_fusion = (bf16[4,10,256,512]{3,2,1,0:T(8,128)(2,1)S(1)}, bf16[4,10,256,512]{3,2,1,0:T(8,128)(2,1)}) fusion(bf16[10,4,256,512]{3,2,1,0:T(8,128)(2,1)} %gather_fusion.3, bf16[10,4,256,512]{3,2,1,0:T(8,128)(2,1)} %gather_fusion.2), kind=kLoop, calls=%fused_computation.10 | loop fusion | bytes 41943040 | tf_op jit(solution)/shard_map/gather | solution.py:53
  139.5 0.0 slice-done
  139.5 0.0 slice-done.1
  139.5 10.5 %fusion.8 = bf16[4,10,128,512]{3,2,1,0:T(8,128)(2,1)} fusion(bf16[4,10,256,512]{3,2,1,0:T(8,128)(2,1)S(1)} %get-tuple-element.7, bf16[4,10,256,512]{3,2,1,0:T(8,128)(2,1)} %get-tuple-element.8, bf16[10,4,128,512]{3,2,1,0:T(8,128)(2,1)S(1)} %bitcast.40), kind=kOutput, calls=%fused_computation.17 | convolution fusion | flops 2728919040 | bytes 31457280 | tf_op jit(solution)/shard_map/fprw,fpcw->fprc/dot_general | solution.py:54
  150.0 7.2 %gather_fusion.1 = bf16[40,128,512]{2,1,0:T(8,128)(2,1)} fusion(bf16[40,128,512]{2,1,0:T(8,128)(2,1)} %bitcast.41, s32[1024]{0:T(1024)S(1)} %pad_clamp_fusion), kind=kCustom, calls=%fused_computation.1 | custom fusion | bytes 10485920 | tf_op jit(solution)/shard_map/gather | solution.py:29
  157.2 5.3 %broadcast_select_fusion = bf16[40,128,512]{2,1,0:T(8,128)(2,1)} fusion(bf16[40,128,512]{2,1,0:T(8,128)(2,1)} %gather_fusion.1, pred[40]{0:T(512)(128)(4,1)S(1)} %iota_compare_fusion.2), kind=kLoop, calls=%fused_computation.16 | loop fusion | flops 2621440 | bytes 10485800 | tf_op jit(solution)/shard_map/jit(_where)/select_n | solution.py:30
  162.4 4.2 %broadcast_in_dim.30 = bf16[64,128,512]{2,1,0:T(8,128)(2,1)} broadcast(bf16[]{:T(256)} %constant.10.clone.1), dimensions={} | broadcast | bytes 8388610 | tf_op jit(solution)/shard_map/broadcast_in_dim | solution.py:32
  166.7 14.1 %scatter_fusion = bf16[64,128,512]{2,1,0:T(8,128)(2,1)} fusion(bf16[64,128,512]{2,1,0:T(8,128)(2,1)} %broadcast_in_dim.30, s32[40]{0:T(128)S(1)} %fusion.17, bf16[40,128,512]{2,1,0:T(8,128)(2,1)} %broadcast_select_fusion), kind=kCustom, calls=%fused_computation.5 | custom fusion | bytes 15728800 | tf_op jit(solution)/shard_map/scatter | solution.py:34
  180.7 0.0 all-to-all-done
  180.7 11.0 %all-to-all-start.1 = ((bf16[64,1,128,512]{3,2,1,0:T(8,128)(2,1)}), bf16[64,1,128,512]{3,2,1,0:T(8,128)(2,1)}, u32[]{:S(2)}, u32[]{:S(2)}) async-start(bf16[64,1,128,512]{3,2,1,0:T(8,128)(2,1)} %bitcast.36), calls=%async_computation.1 | async-start | bytes 16777216 | tf_op jit(solution)/shard_map/all_to_all | solution.py:73
  191.7 0.0 copy-start
  191.7 1.2 reduce
  193.0 184.5 %all-to-all-done.1 = bf16[64,1,128,512]{3,2,1,0:T(8,128)(2,1)} async-done(((bf16[64,1,128,512]{3,2,1,0:T(8,128)(2,1)}), bf16[64,1,128,512]{3,2,1,0:T(8,128)(2,1)}, u32[]{:S(2)}, u32[]{:S(2)}) %all-to-all-start.1) | async-done | bytes 8388640 | tf_op jit(solution)/shard_map/all_to_all | solution.py:73
  377.5 12.3 %fusion.4 = f32[4,128,512]{2,0,1:T(4,128)S(1)} fusion(bf16[64,1,128,512]{3,2,1,0:T(8,128)(2,1)} %all-to-all-done.1, s32[64]{0:T(128)S(1)} %reduce), kind=kOutput, calls=%fused_computation.12 | convolution fusion | flops 33554688 | bytes 9437440 | tf_op jit(solution)/shard_map/tn,nrc->trc/dot_general | solution.py:45
  389.7 0.0 copy-done
  389.7 1.4 copy_subtract_fusion
  (5 shorter events, 0.0 us)
Async XLA Ops:
  6.5 24.6 %copy-start.1 = (s32[10]{0:T(128)S(1)}, s32[10]{0:T(128)}, u32[]{:S(2)}) copy-start(s32[10]{0:T(128)} %constant.35) | copy-start | bytes 124
  6.5 24.6 %copy-start.2 = (s32[1,40]{1,0:T(1,128)S(1)}, s32[1,40]{1,0:T(1,128)}, u32[]{:S(2)}) copy-start(s32[1,40]{1,0:T(1,128)} %param.12) | copy-start | bytes 484
  6.5 91.9 %all-gather.3.cloned.1.call-start = ((), (), s32[]{:S(2)}) async-start(), calls=%async_computation.2 | async-start | bytes 10485760 | tf_op jit(solution)/shard_map/all_gather | solution.py:9
  11.1 169.6 %all-to-all-start = ((s32[64,1,1]{2,1,0:T(1,128)}), s32[64,1,1]{2,1,0:T(1,128)S(1)}, u32[]{:S(2)}, u32[]{:S(2)}) async-start(s32[64,1,1]{2,1,0:T(1,128)} %copy.45), calls=%async_computation | async-start | bytes 65536 | tf_op jit(solution)/shard_map/all_to_all | solution.py:74
  119.5 20.0 %slice-start = ((s8[5242880]{0:T(1024)(128)(4,1)}), s8[1048576]{0:T(1024)(128)(4,1)S(1)}, s32[]{:S(2)}) async-start(s8[5242880]{0:T(1024)(128)(4,1)} %bitcast.39), calls=%async_computation.3 | async-start | bytes 2097152
  127.1 12.4 %slice-start.1 = ((s8[5242880]{0:T(1024)(128)(4,1)}), s8[4194304]{0:T(1024)(128)(4,1)S(1)}, s32[]{:S(2)}) async-start(s8[5242880]{0:T(1024)(128)(4,1)} %bitcast.39), calls=%async_computation.4 | async-start | bytes 8388608
  180.7 196.7 %all-to-all-start.1 = ((bf16[64,1,128,512]{3,2,1,0:T(8,128)(2,1)}), bf16[64,1,128,512]{3,2,1,0:T(8,128)(2,1)}, u32[]{:S(2)}, u32[]{:S(2)}) async-start(bf16[64,1,128,512]{3,2,1,0:T(8,128)(2,1)} %bitcast.36), calls=%async_computation.1 | async-start | bytes 16777216 | tf_op jit(solution)/shard_map/all_to_all | solution.py:73
  191.7 198.0 %copy-start = (f32[4,128,512]{2,1,0:T(8,128)S(1)}, f32[4,128,512]{2,1,0:T(8,128)}, u32[]{:S(2)}) copy-start(f32[4,128,512]{2,1,0:T(8,128)} %param.11) | copy-start | bytes 3145732
Sparse Core Ops, SparseCore 0:
  9.1 89.2 all-gather.2
